TPU v7x, 16 devices: a 4x2x1 block of a 4x4x8 slice. The times are simulated.
16 devices in a mesh: dp: 2 (over y, z), tp: 8 (over x, core).
Axes of the slice: x: 4, y: 2, z: 1, core: 2. Of those that a mesh axis runs over, the one named last changes fastest.
The devices are a block of a 4x4x8 slice.
Arguments:
- x_resid: bfloat16 [64, 512, 2560], P('dp', 'tp'), parts along dimension 0
- positions: int32 [64, 512], P('dp', 'tp'), parts along dimension 0
- norm_gain: bfloat16 [2560], replicated
- w_q: bfloat16 [2560, 4096], P(None, 'tp')
- w_k: bfloat16 [2560, 1024], P(None, 'tp')
- w_v: bfloat16 [2560, 1024], P(None, 'tp')
- q_gain: bfloat16 [128], replicated
- k_gain: bfloat16 [128], replicated
- w_o: bfloat16 [4096, 2560], P('tp')
Outputs:
- output: bfloat16 [64, 512, 2560], P('dp', 'tp'), parts along dimension 0
There are 2 independent parts. A program takes and returns all parts, laid end to end along the dimension named above; an argument that names none is the same for every part.
All inputs are finite; a program needn't handle non-finite values.
Results may differ from a plain program's by a relative error of at most 0.012307.
Values are sent between devices in bfloat16 or wider.
A program may use at most 768 MiB of HBM per device.

v0:
```python
import jax
import jax.numpy as jnp
from jax import lax
from jax.sharding import PartitionSpec as P

EPS = 1e-6
THETA = 1000000.0


def rms_scale(vals, gain):
    mean_sq = jnp.mean(vals * vals, axis=-1, keepdims=True)
    return vals * lax.rsqrt(mean_sq + EPS) * gain.astype(jnp.float32)


def rope_tables(pos_vals, head_dim):
    inv_freq = THETA ** (-(jnp.arange(head_dim // 2, dtype=jnp.float32) * (2.0 / head_dim)))
    angles = pos_vals.astype(jnp.float32)[..., None] * inv_freq
    return jnp.cos(angles), jnp.sin(angles)


def norm_rope(proj, gain, cos_t, sin_t):
    vals = rms_scale(proj.astype(jnp.float32), gain)
    half_dim = vals.shape[-1] // 2
    lower_half = vals[..., :half_dim]
    upper_half = vals[..., half_dim:]
    return jnp.concatenate([lower_half * cos_t - upper_half * sin_t, upper_half * cos_t + lower_half * sin_t], axis=-1).astype(jnp.bfloat16)


def causal_attention(q_rot, k_rot, v_proj, num_blocks):
    block_len = q_rot.shape[1] // num_blocks
    score_scale = q_rot.shape[-1] ** -0.5
    pieces = []
    for block_idx in range(num_blocks):
        key_len = (block_idx + 1) * block_len
        q_block = q_rot[:, block_idx * block_len:key_len]
        scores = jnp.einsum('bqkgh,btkh->bkgqt', q_block, k_rot[:, :key_len], preferred_element_type=jnp.float32) * score_scale
        query_index = block_idx * block_len + jnp.arange(block_len)
        allowed = query_index[:, None] >= jnp.arange(key_len)[None, :]
        scores = jnp.where(allowed, scores, -jnp.inf)
        peak_val = jnp.max(scores, axis=-1, keepdims=True)
        exp_scores = jnp.exp(scores - peak_val)
        attn_probs = (exp_scores / jnp.sum(exp_scores, axis=-1, keepdims=True)).astype(jnp.bfloat16)
        mixed = jnp.einsum('bkgqt,btkh->bqkgh', attn_probs, v_proj[:, :key_len], preferred_element_type=jnp.float32)
        pieces.append(mixed.astype(jnp.bfloat16))
    return jnp.concatenate(pieces, axis=1)


def local_heads(full_normed, full_pos, w_q, w_k, w_v, q_gain, k_gain, w_o, num_blocks):
    batch_size = full_normed.shape[0]
    seq_len = full_normed.shape[1]
    head_dim = q_gain.shape[0]
    kv_local = w_k.shape[1] // head_dim
    group_size = w_q.shape[1] // w_k.shape[1]
    q_proj = jnp.einsum('bsd,df->bsf', full_normed, w_q, preferred_element_type=jnp.float32).astype(jnp.bfloat16).reshape(batch_size, seq_len, kv_local, group_size, head_dim)
    k_proj = jnp.einsum('bsd,df->bsf', full_normed, w_k, preferred_element_type=jnp.float32).astype(jnp.bfloat16).reshape(batch_size, seq_len, kv_local, head_dim)
    v_proj = jnp.einsum('bsd,df->bsf', full_normed, w_v, preferred_element_type=jnp.float32).astype(jnp.bfloat16).reshape(batch_size, seq_len, kv_local, head_dim)
    cos_t, sin_t = rope_tables(full_pos, head_dim)
    q_rot = norm_rope(q_proj, q_gain, cos_t[:, :, None, None, :], sin_t[:, :, None, None, :])
    k_rot = norm_rope(k_proj, k_gain, cos_t[:, :, None, :], sin_t[:, :, None, :])
    attn_out = causal_attention(q_rot, k_rot, v_proj, num_blocks).reshape(batch_size, seq_len, -1)
    return jnp.einsum('bsf,fd->bsd', attn_out, w_o, preferred_element_type=jnp.float32).astype(jnp.bfloat16)


def solution(mesh):
    tp_size = mesh.shape['tp']

    def local_block(x_loc, pos_loc, norm_gain, w_q, w_k, w_v, q_gain, k_gain, w_o):
        x_f32 = x_loc.astype(jnp.float32)
        normed = rms_scale(x_f32, norm_gain).astype(jnp.bfloat16)
        full_normed = lax.all_gather(normed, 'tp', axis=1, tiled=True)
        full_pos = lax.all_gather(pos_loc, 'tp', axis=1, tiled=True)
        head_partial = local_heads(full_normed, full_pos, w_q, w_k, w_v, q_gain, k_gain, w_o, tp_size)
        summed = lax.psum_scatter(head_partial, 'tp', scatter_dimension=1, tiled=True)
        return (x_f32 + summed.astype(jnp.float32)).astype(jnp.bfloat16)

    return jax.shard_map(local_block, mesh=mesh, in_specs=(P('dp', 'tp', None), P('dp', 'tp'), P(None), P(None, 'tp'), P(None, 'tp'), P(None, 'tp'), P(None), P(None), P('tp', None)), out_specs=P('dp', 'tp', None), check_vma=False)
```

profile of v0, /device:TPU:113, one launch (start us, length us, event | category | flops | bytes accessed | tf_op | source)
XLA Modules:
  0.0 1305.5 jit_solution(16388417649502961191)
XLA Ops:
  6.6 0.8 convert_element_type.174
  7.4 6.1 fusion
  13.5 10.8 fusion.2
  24.3 0.1 all-gather.3.cloned.1.call-update
  24.4 0.1 reduce-scatter.2.cloned.1.call-start
  24.5 0.5 copy-done.31
  25.0 0.0 copy-done.32
  25.0 0.1 copy-done.30
  25.1 19.0 %all-gather = s32[8,64,32]{1,2,0:T(8,128)S(1)} all-gather(s32[1,64,32]{1,2,0:T(8,128)S(1)} %bitcast.408), channel_id=1, replica_groups=mesh['dp'=2,'tp'=8] {'tp'}, dimensions={0}, use_global_device_ids=true | all-gather | bytes 73728 | tf_op jit(solution)/shard_map/all_gather | solution.py:71
  44.1 0.1 copy.38
  44.2 0.1 reshape.442
  44.3 0.6 iota_compare_fusion.7
  44.9 0.7 iota_compare_fusion.6
  45.6 0.7 iota_compare_fusion.4
  46.3 0.7 iota_compare_fusion.5
  47.0 0.7 iota_compare_fusion.2
  47.7 0.7 iota_compare_fusion.3
  48.3 0.7 iota_compare_fusion
  49.0 0.7 iota_compare_fusion.1
  49.7 31.9 %multiply_cosine_fusion = (f32[32,512,64]{2,1,0:T(8,128)}, f32[32,512,64]{2,1,0:T(8,128)}) fusion(f32[64]{0:T(128)S(1)} %negate_power_fusion, f32[32,512]{1,0:T(8,128)S(1)} %bitcast.406), kind=kLoop, calls=%fused_computation.29 | loop fusion | flops 1048576 | bytes 8454400 | tf_op jit(solution)/shard_map/cos | solution.py:18
  81.7 310.4 %all-gather.3.cloned.1.call-done = bf16[32,512,2560]{2,1,0:T(8,128)(2,1)} async-done(((bf16[32,64,2560]{2,1,0:T(8,128)(2,1)}), bf16[32,512,2560]{2,1,0:T(8,128)(2,1)}) %all-gather.3.cloned.1.call-update) | async-done | bytes 83886096 | tf_op jit(solution)/shard_map/all_gather | solution.py:70
  392.1 51.5 %convolution_convert_fusion.1 = bf16[32,512,512]{1,2,0:T(8,128)(2,1)} fusion(bf16[32,512,2560]{2,1,0:T(8,128)(2,1)} %all-gather.3.cloned.1.call-done, bf16[2560,512]{1,0:T(8,128)(2,1)} %param.12), kind=kOutput, calls=%fused_computation.34 | convolution fusion | flops 42958061568 | bytes 103284736 | tf_op jit(solution)/shard_map/bsd,df->bsf/dot_general | solution.py:54
  443.6 7.2 multiply_reduce_fusion
  450.8 0.0 copy-start.8
  450.8 23.8 %copy.40 = f32[32,512,1,4,128]{4,1,3,0,2:T(8,128)} copy(bf16[32,512,1,4,128]{1,4,3,0,2:T(8,128)(2,1)} %bitcast.394) | data formatting | bytes 50331648 | tf_op jit(solution)/shard_map/convert_element_type | solution.py:22
  474.6 49.0 %fusion.12 = (f32[32,512]{1,0:T(8,128)}, bf16[32,512,128]{1,2,0:T(8,128)(2,1)}) fusion(bf16[32,512,2560]{2,1,0:T(8,128)(2,1)} %all-gather.3.cloned.1.call-done, bf16[2560,128]{1,0:T(8,128)(2,1)S(1)} %copy-done.8), kind=kOutput, calls=%fused_computation.37 | convolution fusion | flops 10745790464 | bytes 88801280 | tf_op jit(solution)/shard_map/bsd,df->bsf/dot_general | solution.py:55
  523.6 0.9 add_rsqrt_fusion.1
  524.5 0.1 add_rsqrt_fusion
  524.6 3.6 fusion.14
  528.2 17.2 %fusion.38 = (bf16[32,512,1,64]{1,3,0,2:T(8,128)(2,1)}, bf16[32,512,1,64]{1,3,0,2:T(8,128)(2,1)}) fusion(f32[32,512,1,128]{1,3,0,2:T(8,128)S(1)} %fusion.14, f32[64]{0:T(128)S(1)} %negate_power_fusion, f32[32,512]{1,0:T(8,128)S(1)} %bitcast.407), kind=kLoop, calls=%fused_computation.97 | loop fusion | flops 9437184 | bytes 12648704 | tf_op jit(solution)/shard_map/convert.8
  545.4 23.0 %multiply_multiply_fusion = f32[32,512,1,4,128]{4,1,3,0,2:T(8,128)} fusion(f32[32,512,1,4,128]{4,1,3,0,2:T(8,128)} %copy.40, f32[128]{0:T(128)S(1)} %convert_element_type.184, f32[32,512,4]{1,2,0:T(4,128)S(1)} %add_rsqrt_fusion), kind=kLoop, calls=%fused_computation.3 | loop fusion | flops 16777216 | bytes 67371520 | tf_op jit(solution)/shard_map/mul | solution.py:12
  568.4 34.4 %add_convert_fusion = (bf16[32,512,1,4,64]{4,1,3,0,2:T(8,128)(2,1)S(1)}, bf16[32,512,1,4,64]{4,1,3,0,2:T(8,128)(2,1)}) fusion(f32[32,512,1,4,128]{4,1,3,0,2:T(8,128)} %multiply_multiply_fusion, f32[32,512,64]{2,1,0:T(8,128)} %get-tuple-element.10, f32[32,512,64]{2,1,0:T(8,128)} %get-tuple-element.9), kind=kLoop, calls=%fused_computation.1 | loop fusion | flops 33554432 | bytes 58720256 | tf_op jit(solution)/shard_map/convert.6
  602.9 9.5 fusion.55
  612.3 5.6 fusion.56
  617.9 7.2 fusion.23
  625.2 7.0 fusion.24
  632.2 11.5 fusion.10
  643.8 0.0 slice-start.10
  643.8 7.8 fusion.11
  651.6 0.0 slice-start.11
  651.6 10.7 fusion.6
  662.4 4.2 fusion.53
  666.7 4.8 fusion.54
  671.4 3.7 fusion.21
  675.2 3.6 fusion.22
  678.8 33.6 %convolution_convert_fusion.3 = bf16[32,512,128]{2,1,0:T(8,128)(2,1)} fusion(bf16[32,512,2560]{2,1,0:T(8,128)(2,1)} %all-gather.3.cloned.1.call-done, bf16[2560,128]{1,0:T(8,128)(2,1)} %param.14), kind=kOutput, calls=%fused_computation.132 | convolution fusion | flops 10739515392 | bytes 88735744 | tf_op jit(solution)/shard_map/bsd,df->bsf/dot_general | solution.py:56
  712.4 5.2 bitcast_dynamic-update-slice_fusion.7
  717.7 3.9 bitcast_dynamic-update-slice_fusion.6
  721.6 7.8 bitcast_dynamic-update-slice_fusion.5
  729.4 5.6 bitcast_dynamic-update-slice_fusion.4
  735.1 3.8 fusion.8
  738.9 8.3 bitcast_dynamic-update-slice_fusion.3
  747.2 4.1 fusion.9
  751.4 8.2 bitcast_dynamic-update-slice_fusion.2
  759.6 10.5 fusion.7
  770.1 8.0 fusion.5
  778.2 8.1 fusion.4
  786.2 9.4 bitcast_dynamic-update-slice_fusion.1
  795.7 9.7 bitcast_dynamic-update-slice_fusion
  805.4 22.6 %copy.50 = bf16[32,512,1,4,128]{1,4,3,0,2:T(8,128)(2,1)} copy(bf16[32,512,1,4,128]{4,1,3,0,2:T(8,128)(2,1)} %bitcast_dynamic-update-slice_fusion) | data formatting | bytes 33554432 | tf_op jit(solution)/shard_map/concatenate | solution.py:45
  827.9 55.6 %convolution_convert_fusion = bf16[32,512,2560]{2,1,0:T(8,128)(2,1)} fusion(bf16[32,512,512]{1,2,0:T(8,128)(2,1)} %bitcast.405, bf16[512,2560]{1,0:T(8,128)(2,1)S(1)} %copy-done), kind=kOutput, calls=%fused_computation | convolution fusion | flops 42991616000 | bytes 103284736 | tf_op jit(solution)/shard_map/bsf,fd->bsd/dot_general | solution.py:61
  883.5 0.1 reduce-scatter.2.cloned.1.call-update
  883.6 401.0 %reduce-scatter.2.cloned.1.call-done = bf16[32,64,2560]{2,1,0:T(8,128)(2,1)} async-done(((bf16[32,512,2560]{2,1,0:T(8,128)(2,1)}), bf16[32,64,2560]{2,1,0:T(8,128)(2,1)}) %reduce-scatter.2.cloned.1.call-update) | async-done | bytes 10485776 | tf_op jit(solution)/shard_map/reduce_scatter | solution.py:73
  1284.6 13.8 %fusion.3 = bf16[32,64,2560]{2,1,0:T(8,128)(2,1)} fusion(bf16[32,64,2560]{2,1,0:T(8,128)(2,1)} %param.9, bf16[32,64,2560]{2,1,0:T(8,128)(2,1)} %reduce-scatter.2.cloned.1.call-done), kind=kLoop, calls=%fused_computation.11 | loop fusion | flops 20971520 | bytes 31457280 | tf_op jit(solution)/shard_map/convert_element_type | solution.py:74
  (106 shorter events, 0.2 us)
Async XLA Ops:
  6.5 821.4 %copy-start = (bf16[512,2560]{1,0:T(8,128)(2,1)S(1)}, bf16[512,2560]{1,0:T(8,128)(2,1)}, u32[]{:S(2)}) copy-start(bf16[512,2560]{1,0:T(8,128)(2,1)} %param.17) | copy-start | bytes 7864324
  6.6 385.6 %all-gather.3.cloned.1.call-start = ((), (), s32[]{:S(2)}) async-start(), calls=%async_computation.1 | async-start | bytes 94371840 | tf_op jit(solution)/shard_map/all_gather | solution.py:70
  24.3 0.7 copy-start.31
  24.3 0.7 copy-start.32
  24.3 0.7 copy-start.30
  24.4 1260.2 %reduce-scatter.2.cloned.1.call-start = ((), (), s32[]{:S(2)}) async-start(), calls=%async_computation.2 | async-start | bytes 94371840 | tf_op jit(solution)/shard_map/reduce_scatter | solution.py:73
  44.2 37.4 %copy-start.9 = (f32[512,32]{0,1:T(8,128)}, f32[512,32]{0,1:T(8,128)S(1)}, u32[]{:S(2)}) copy-start(f32[512,32]{0,1:T(8,128)S(1)} %reshape.442) | copy-start | bytes 196612
  450.8 23.8 %copy-start.8 = (bf16[2560,128]{1,0:T(8,128)(2,1)S(1)}, bf16[2560,128]{1,0:T(8,128)(2,1)}, u32[]{:S(2)}) copy-start(bf16[2560,128]{1,0:T(8,128)(2,1)} %param.13) | copy-start | bytes 1966084
  523.6 4.6 copy-start.10
  568.4 34.4 %copy-start.25 = (pred[64,64]{0,1:T(8,128)(4,1)S(1)}, pred[64,64]{0,1:T(8,128)(4,1)}, u32[]{:S(2)}) copy-start(pred[64,64]{0,1:T(8,128)(4,1)} %iota_compare_fusion.7) | copy-start | bytes 12292
  602.8 22.3 %copy-start.1 = (bf16[32,512,1,4,64]{4,1,3,0,2:T(8,128)(2,1)}, bf16[32,512,1,4,64]{4,1,3,0,2:T(8,128)(2,1)S(1)}, u32[]{:S(2)}) copy-start(bf16[32,512,1,4,64]{4,1,3,0,2:T(8,128)(2,1)S(1)} %get-tuple-element.5) | copy-start | bytes 25165828
  602.8 9.5 copy-start.2
  602.8 9.5 copy-start.4
  602.8 9.5 copy-start.24
  612.3 5.6 copy-start.21
  617.9 7.2 copy-start.18
  625.2 7.0 copy-start.17
  632.2 11.6 copy-start.3
  632.2 11.6 copy-start.5
  632.2 11.6 copy-start.16
  643.8 7.8 copy-start.12
  643.8 27.6 %slice-start.10 = ((s8[8388608]{0:T(1024)(128)(4,1)}), s8[4194304]{0:T(1024)(128)(4,1)S(1)}, s32[]{:S(2)}) async-start(s8[8388608]{0:T(1024)(128)(4,1)} %bitcast.403), calls=%async_computation.13 | async-start | bytes 8388608
  651.6 10.8 copy-start.15
  651.6 10.8 copy-start.26
  651.6 15.0 %copy-start.13 = (f32[32,4,64]{2,1,0:T(4,128)S(1)}, f32[32,4,64]{2,1,0:T(4,128)}, u32[]{:S(2)}) copy-start(f32[32,4,64]{2,1,0:T(4,128)} %get-tuple-element.15) | copy-start | bytes 98308
  651.6 19.8 %slice-start.11 = ((s8[8388608]{0:T(1024)(128)(4,1)}), s8[4194304]{0:T(1024)(128)(4,1)S(1)}, s32[]{:S(2)}) async-start(s8[8388608]{0:T(1024)(128)(4,1)} %bitcast.403), calls=%async_computation.14 | async-start | bytes 8388608
  662.4 9.0 copy-start.22
  662.4 12.7 slice-start.6
  662.4 12.7 copy-start.19
  666.6 8.5 slice-start.7
  712.4 5.2 copy-start.7
  712.4 5.2 copy-start.14
  712.4 5.2 copy-start.29
  712.4 5.2 copy-start.33
  717.6 3.9 copy-start.23
  717.6 3.9 copy-start.28
  717.6 11.8 slice-start.8
  721.5 7.9 slice-start.9
  721.5 7.9 copy-start.20
  721.5 7.9 copy-start.27
  721.5 13.5 %slice-start.3 = ((s8[12582912]{0:T(1024)(128)(4,1)}), s8[4194304]{0:T(1024)(128)(4,1)S(1)}, s32[]{:S(2)}) async-start(s8[12582912]{0:T(1024)(128)(4,1)} %bitcast.397), calls=%async_computation.6 | async-start | bytes 8388608
  721.6 13.5 %slice-start.4 = ((s8[12582912]{0:T(1024)(128)(4,1)}), s8[4194304]{0:T(1024)(128)(4,1)S(1)}, s32[]{:S(2)}) async-start(s8[12582912]{0:T(1024)(128)(4,1)} %bitcast.397), calls=%async_computation.7 | async-start | bytes 8388608
  729.4 5.6 slice-start.5
  735.0 12.2 slice-start
  738.9 8.3 slice-start.1
  738.9 8.3 slice-start.2
  747.2 4.1 copy-start.34
  751.3 8.2 copy-start.6
  751.4 8.2 copy-start.11
Sparse Core Ops, SparseCore 0:
  24.5 367.5 all-gather.2
  883.7 400.8 reduce-scatter.1
where the time goes:
time: 1310 us
  waiting for transfers between devices  712 us (54%)
  matrix products  318 us (24%)
  other arithmetic  196 us (15%)
  local copies, waits for them, and re-layouts  47.3 us (4%)
  blocking collectives  19 us (1%)
  between operations  14.3 us (1%)
    reduce_scatter x1, waiting for transfers between devices, local_block(): lax.psum_scatter(head_partial, 'tp', scatter_dimension=1, tiled=True)  401 us
    all_gather x1, waiting for transfers between devices, local_block(): full_normed = lax.all_gather(normed, 'tp', axis=1, tiled=True)  310 us
    dot_general x8, matrix products, causal_attention(): jnp.einsum('bqkgh,btkh->bkgqt', q_block, k_rot[:, :key_len], preferred_el...  69.8 us
    dot_general x8, matrix products, causal_attention(): jnp.einsum('bkgqt,btkh->bqkgh', attn_probs, v_proj[:, :key_len], preferre...  58.1 us
    dot_general x1, matrix products, local_heads(): jnp.einsum('bsf,fd->bsd', attn_out, w_o, preferred_element_type=jnp.float32)  55.6 us
    another operation x2, other arithmetic  51.6 us
    dot_general x1, matrix products, local_heads(): jnp.einsum('bsd,df->bsf', full_normed, w_q, preferred_element_type=jnp.fl...  51.5 us
    dot_general x1, matrix products, local_heads(): jnp.einsum('bsd,df->bsf', full_normed, w_k, preferred_element_type=jnp.fl...  49 us
  transfers between devices with their start and end apart: 2, of which 2 were waited for; matrix products, arithmetic and copies ran while one was open for 3% of the time, Pallas kernels for 0%

commit v1 on v0

v1 whole, which is shorter than its diff:
```python
import functools

import jax
import jax.numpy as jnp
from jax import lax
from jax.experimental import pallas as pl
from jax.experimental.pallas import tpu as pltpu
from jax.sharding import PartitionSpec as P

EPS = 1e-6
THETA = 1000000.0
MESH = pl.DeviceIdType.MESH
LOG2E = 1.4426950408889634


def body(x_in, pos_in, invf, ngain, qgain, kgain, wq_in, wk_in, wv_in, wo_in,
         out, wq_all, wk_all, wv_all, wo_all, xrel, yrel,
         xbuf, nbuf, obuf, wbuf, wobuf, qkvb, qs, ks, cosb, sinb, posbuf, posrel,
         a_send, a_recv, r_recv, w_own, w_fwd, w_sib, w_recv, w_loc, ld_sem, wo_sem):
    d_model = nbuf.shape[1]
    seq = nbuf.shape[0]
    n_seq = xbuf.shape[0]
    hd = ks.shape[1]
    n_heads = qs.shape[0]
    q_cols = n_heads * hd
    n_tp = wq_all.shape[0]
    chips = n_tp // 2
    piece = seq // n_tp
    dp_i = lax.axis_index('dp')
    me = lax.axis_index('tp')
    chip = me // 2
    core = me % 2

    def dev(dc, dk):
        return ((chip + dc + chips) % chips) * 2 + (core + dk) % 2

    def dev_abs(dc, k_abs):
        return ((chip + dc + chips) % chips) * 2 + k_abs

    sib = dev(0, 1)

    def rcopy(src, dst, ssem, rsem, target):
        return pltpu.make_async_remote_copy(src_ref=src, dst_ref=dst, send_sem=ssem, recv_sem=rsem,
                                            device_id=(dp_i, target), device_id_type=MESH)

    bar = pltpu.get_barrier_semaphore()
    near = [sib, dev_abs(1, 0), dev_abs(1, 1), dev_abs(-1, 0), dev_abs(-1, 1)]
    for t in near:
        pl.semaphore_signal(bar, inc=1, device_id=(dp_i, t), device_id_type=MESH)
    pl.semaphore_wait(bar, len(near))

    def rows(r):
        return pl.ds(pl.multiple_of(r * piece, piece), piece)

    def a2a_direct(a, src, dst, rel):
        far0, far1 = dev_abs(2, 0), dev_abs(2, 1)
        right, left = dev(1, 0), dev(-1, 0)
        return [
            rcopy(src(far0), rel(0), a_send.at[a, 0], r_recv.at[a, 0], right),
            rcopy(src(far1), rel(1), a_send.at[a, 1], r_recv.at[a, 1], left),
            rcopy(src(near[1]), dst(me, near[1]), a_send.at[a, 2], a_recv.at[a, me], near[1]),
            rcopy(src(near[3]), dst(me, near[3]), a_send.at[a, 3], a_recv.at[a, me], near[3]),
            rcopy(src(near[2]), dst(me, near[2]), a_send.at[a, 4], a_recv.at[a, me], near[2]),
            rcopy(src(near[4]), dst(me, near[4]), a_send.at[a, 5], a_recv.at[a, me], near[4]),
            rcopy(src(sib), dst(me, sib), a_send.at[a, 6], a_recv.at[a, me], sib),
        ]

    def a2a_local(a, src, dst):
        return pltpu.make_async_copy(src(me), dst(me, me), a_recv.at[a, me])

    def a2a_relay(a, dst, rel):
        s0, s1 = dev(-1, 0), dev(1, 0)
        return [
            rcopy(rel(0), dst(s0, near[1]), a_send.at[a, 7], a_recv.at[a, s0], near[1]),
            rcopy(rel(1), dst(s1, near[4]), a_send.at[a, 8], a_recv.at[a, s1], near[4]),
        ]

    def a2a_start(a, src, dst, rel):
        for c in a2a_direct(a, src, dst, rel):
            c.start()
        a2a_local(a, src, dst).start()

    def a2a_forward(a, dst, rel):
        fw = a2a_relay(a, dst, rel)
        for side in range(2):
            rcopy(rel(side), rel(side), a_send.at[a, 7 + side], r_recv.at[a, side], sib).wait_recv()
            fw[side].start()

    def a2a_wait(a, src, dst):
        a2a_local(a, src, dst).wait()
        for dc, dk in ((0, 1), (1, 0), (1, 1), (-1, 0), (-1, 1), (2, 0), (2, 1)):
            r = dev(dc, dk)
            ref = dst(r, me)
            rcopy(ref, ref, a_send.at[a, 0], a_recv.at[a, r], sib).wait_recv()

    def a2a_wait_sends(a, src, dst, rel):
        for c in a2a_direct(a, src, dst, rel) + a2a_relay(a, dst, rel):
            c.wait_send()

    def pos_src(r):
        return pos_in.at[r]

    def pos_dst(r, to):
        return posbuf.at[rows(r)]

    def pos_rel(side):
        return posrel.at[side]

    def x_fns(j):
        return (lambda r: x_in.at[r * n_seq + j],
                lambda r, to: xbuf.at[j, rows(r)],
                lambda side: xrel.at[j, side])

    def y_fns(j):
        return (lambda r: xbuf.at[j, rows(r)],
                lambda r, to: out.at[r * n_seq + j],
                lambda side: yrel.at[j, side])

    def set_x(j):
        return 1 + j

    def set_y(j):
        return 1 + n_seq + j

    w_in = (wq_in, wk_in, wv_in, wo_in)
    w_all = (wq_all, wk_all, wv_all, wo_all)

    def w_send_own(i, which, target):
        return rcopy(w_in[i], w_all[i].at[me], w_own.at[which, i], w_recv.at[me, i], target)

    def w_wait(i, r):
        ref = w_all[i].at[r]
        rcopy(ref, ref, w_own.at[0, 0], w_recv.at[r, i], sib).wait_recv()

    def w_to_sib(i, r, slot):
        return rcopy(w_all[i].at[r], w_all[i].at[r], w_sib.at[slot, i], w_recv.at[r, i], sib)

    def w_onward(i, r, target):
        return rcopy(w_all[i].at[r], w_all[i].at[r], w_fwd.at[i], w_recv.at[r, i], target)

    left, right, far = dev(-1, 0), dev(1, 0), dev(2, 0)
    Q, K, V, O = range(4)

    a2a_start(0, pos_src, pos_dst, pos_rel)
    a2a_start(set_x(0), *x_fns(0))
    for i in range(4):
        w_send_own(i, 0, sib).start()
    w_local = [pltpu.make_async_copy(w_in[i], w_all[i].at[me], w_loc.at[i]) for i in range(4)]
    a2a_forward(0, pos_dst, pos_rel)
    a2a_forward(set_x(0), *x_fns(0)[1:])
    for i in (Q, K, O, V):
        w_send_own(i, 1, right).start()
    for i in (O, V, Q, K):
        w_send_own(i, 2, left).start()
    for c in w_local:
        c.start()
    a2a_wait(0, pos_src, pos_dst)

    lane = lax.broadcasted_iota(jnp.int32, (piece, hd), 1)

    def table_step(r, _):
        rs = rows(r)
        for j in range(n_seq):
            ang = posbuf[rs, j:j + 1] * invf[...]
            cosb[j, rs, :] = jnp.cos(ang)
            sn = jnp.sin(ang)
            sinb[j, rs, :] = jnp.where(lane < hd // 2, -sn, sn)
        return 0

    lax.fori_loop(0, n_tp, table_step, 0)

    def gid(s):
        m = s // 2
        return ((chip + (3 * m * (m + 1) // 2)) % chips) * 2 + (core + s) % 2

    cols = ((Q, 0, q_cols), (K, q_cols, hd), (V, q_cols + hd, hd))

    def load_w(g, slot):
        return [pltpu.make_async_copy(w_all[i].at[g], wbuf.at[slot, :, c0:c0 + cn], ld_sem.at[slot, i])
                for i, c0, cn in cols]

    def load_own(slot):
        return [pltpu.make_async_copy(w_in[i], wbuf.at[slot, :, c0:c0 + cn], ld_sem.at[slot, i])
                for i, c0, cn in cols]

    nt_cols = wobuf.shape[3]
    n_nt = d_model // nt_cols

    def load_wo(nt, slot):
        return pltpu.make_async_copy(wo_all.at[:, :, pl.ds(pl.multiple_of(nt * nt_cols, nt_cols), nt_cols)],
                                     wobuf.at[slot], wo_sem.at[slot])

    scale2 = (hd ** -0.5) * LOG2E
    blk = 128
    n_blk = seq // blk
    rmod = lax.broadcasted_iota(jnp.int32, (n_heads, blk, blk), 1)
    cmod = lax.broadcasted_iota(jnp.int32, (n_heads, blk, blk), 2)
    tri = (rmod >= cmod).reshape(n_heads * blk, blk)

    def norm_rope(u, gain, cs, sn):
        u = u.astype(jnp.float32)
        ms = jnp.mean(u * u, axis=-1, keepdims=True)
        w = u * lax.rsqrt(ms + EPS) * gain
        return (w * cs + pltpu.roll(w, hd // 2, 1) * sn).astype(jnp.bfloat16)

    def unit(j, g, slot):
        qkvb[...] = jnp.dot(nbuf[...], wbuf[slot], preferred_element_type=jnp.float32).astype(jnp.bfloat16)

        def rope_step(b, _):
            rs = pl.ds(pl.multiple_of(b * 64, 64), 64)
            cs, sn = cosb[j, rs, :], sinb[j, rs, :]
            for h in range(n_heads):
                qs[h, rs, :] = norm_rope(qkvb[rs, h * hd:(h + 1) * hd], qgain[...], cs, sn)
            ks[rs, :] = norm_rope(qkvb[rs, q_cols:q_cols + hd], kgain[...], cs, sn)
            return 0

        lax.fori_loop(0, seq // 64, rope_step, 0)
        ocol = pl.multiple_of(g * q_cols, q_cols)
        for i in range(n_blk):
            kl = (i + 1) * blk
            lhs = qs[:, i * blk:kl, :].reshape(n_heads * blk, hd)
            s = lax.dot_general(lhs, ks[:kl, :], (((1,), (1,)), ((), ())), preferred_element_type=jnp.float32)
            diag = jnp.where(tri, s[:, i * blk:kl], -jnp.inf)
            s = diag if i == 0 else jnp.concatenate([s[:, :i * blk], diag], axis=1)
            peak = jnp.max(s, axis=-1, keepdims=True)
            e = jnp.exp2((s - peak) * scale2)
            inv = 1.0 / jnp.sum(e, axis=-1, keepdims=True)
            p = (e * inv).astype(jnp.bfloat16)
            o = jnp.dot(p, qkvb[:kl, q_cols + hd:q_cols + 2 * hd], preferred_element_type=jnp.float32)
            o = o.astype(jnp.bfloat16)
            for h in range(n_heads):
                obuf[i * blk:kl, pl.ds(pl.multiple_of(ocol + h * hd, hd), hd)] = o[h * blk:(h + 1) * blk]

    n_grp = n_tp
    last = n_seq * n_grp - 1

    def comm_first(s):
        @pl.when(s == 1)
        def _():
            for i in range(4):
                w_wait(i, sib)

        @pl.when(s == 2)
        def _():
            for i in (Q, K):
                w_wait(i, left)
                w_onward(i, left, right).start()
                w_to_sib(i, left, 0).start()
                oi = {Q: O, K: V}[i]
                w_wait(oi, right)
                w_onward(oi, right, left).start()
                w_to_sib(oi, right, 1).start()
            a2a_start(set_x(1), *x_fns(1))
            for i in (O, V):
                w_wait(i, left)
                w_to_sib(i, left, 0).start()
                oi = {O: Q, V: K}[i]
                w_wait(oi, right)
                w_to_sib(oi, right, 1).start()
            for c in w_local:
                c.wait()

        @pl.when(s == 3)
        def _():
            for i in range(4):
                w_wait(i, dev(-1, 1))

        @pl.when(s == 5)
        def _():
            for i in range(4):
                w_wait(i, dev(1, 1))

        @pl.when(s == 6)
        def _():
            for i in (Q, O, K, V):
                w_wait(i, far)
                w_to_sib(i, far, 2).start()

        @pl.when(s == 7)
        def _():
            for i in range(4):
                w_wait(i, dev(2, 1))

    def seq_step(j, _):
        a2a_wait(set_x(j), *x_fns(j)[:2])

        def n_step(r, _):
            rs = rows(r)
            xv = xbuf[j, rs, :].astype(jnp.float32)
            ms = jnp.mean(xv * xv, axis=-1, keepdims=True)
            nbuf[rs, :] = (xv * lax.rsqrt(ms + EPS) * ngain[...]).astype(jnp.bfloat16)
            return 0

        lax.fori_loop(0, n_tp, n_step, 0)

        def grp_step(s, _):
            t = j * n_grp + s
            slot = t % 2

            @pl.when(j == 0)
            def _():
                comm_first(s)

                @pl.when(s == 0)
                def _():
                    for c in load_own(slot):
                        c.start()

                @pl.when(s > 0)
                def _():
                    for c in load_w(gid(s), slot):
                        c.start()

            @pl.when(jnp.logical_and(j > 0, s == 2))
            def _():
                a2a_forward(set_y(j - 1), *y_fns(j - 1)[1:])

            for c in load_w(gid(s), slot):
                c.wait()

            @pl.when(jnp.logical_and(t >= n_grp - 1, t < last))
            def _():
                for c in load_w(gid((s + 1) % n_grp), 1 - slot):
                    c.start()

            @pl.when(s == n_grp - 1)
            def _():
                load_wo(0, 0).start()

                @pl.when(j + 1 < n_seq)
                def _():
                    a2a_forward(set_x(j + 1), *x_fns(j + 1)[1:])

                @pl.when(j + 2 < n_seq)
                def _():
                    a2a_start(set_x(j + 2), *x_fns(j + 2))

            unit(j, gid(s), slot)
            return 0

        lax.fori_loop(0, n_grp, grp_step, 0)

        def out_step(nt, _):
            ws = nt % 2
            load_wo(nt, ws).wait()

            @pl.when(nt + 1 < n_nt)
            def _():
                load_wo(nt + 1, 1 - ws).start()

            cs = pl.ds(pl.multiple_of(nt * nt_cols, nt_cols), nt_cols)
            acc = jnp.dot(obuf[...], wobuf[ws].reshape(n_tp * q_cols, nt_cols), preferred_element_type=jnp.float32)
            xbuf[j, :, cs] = (xbuf[j, :, cs].astype(jnp.float32) + acc).astype(jnp.bfloat16)
            return 0

        lax.fori_loop(0, n_nt, out_step, 0)
        a2a_start(set_y(j), *y_fns(j))
        return 0

    lax.fori_loop(0, n_seq, seq_step, 0)

    a2a_forward(set_y(n_seq - 1), *y_fns(n_seq - 1)[1:])
    for i in range(4):
        w_send_own(i, 0, sib).wait_send()
        w_send_own(i, 1, right).wait_send()
        w_send_own(i, 2, left).wait_send()
    for i in (Q, K):
        w_onward(i, left, right).wait_send()
    for i in (O, V):
        w_onward(i, right, left).wait_send()
    for i in range(4):
        for slot, r in enumerate((left, right, far)):
            w_to_sib(i, r, slot).wait_send()
    a2a_wait_sends(0, pos_src, pos_dst, pos_rel)

    def end_step(j, _):
        a2a_wait_sends(set_x(j), *x_fns(j))
        a2a_wait(set_y(j), *y_fns(j)[:2])
        a2a_wait_sends(set_y(j), *y_fns(j))
        return 0

    lax.fori_loop(0, n_seq, end_step, 0)


def solution(mesh):
    n_tp = mesh.shape['tp']

    def local_block(x_loc, pos_loc, norm_gain, w_q, w_k, w_v, q_gain, k_gain, w_o):
        batch, piece, d_model = x_loc.shape
        hd = q_gain.shape[0]
        q_cols = w_q.shape[1]
        n_heads = q_cols // hd
        n_seq = batch // n_tp
        seq = piece * n_tp
        f32, bf16 = jnp.float32, jnp.bfloat16
        pos = pos_loc.astype(f32).reshape(n_tp, n_seq, piece).transpose(0, 2, 1)
        pos = jnp.pad(pos, ((0, 0), (0, 0), (0, hd - n_seq)))
        inv_freq = THETA ** (-(jnp.arange(hd // 2, dtype=f32) * (2.0 / hd)))
        invf = jnp.concatenate([inv_freq, inv_freq])[None, :]
        any_spec = pl.BlockSpec(memory_space=pl.ANY)
        vmem = pl.BlockSpec(memory_space=pltpu.VMEM)
        nt_cols = 512
        dma = pltpu.SemaphoreType.DMA
        n_sets = 1 + 2 * n_seq
        res = pl.pallas_call(
            body,
            name='attn_block',
            out_shape=[
                jax.ShapeDtypeStruct((batch, piece, d_model), bf16),
                jax.ShapeDtypeStruct((n_tp,) + w_q.shape, bf16),
                jax.ShapeDtypeStruct((n_tp,) + w_k.shape, bf16),
                jax.ShapeDtypeStruct((n_tp,) + w_v.shape, bf16),
                jax.ShapeDtypeStruct((n_tp,) + w_o.shape, bf16),
                jax.ShapeDtypeStruct((n_seq, 2, piece, d_model), bf16),
                jax.ShapeDtypeStruct((n_seq, 2, piece, d_model), bf16),
            ],
            in_specs=[any_spec, any_spec, vmem, vmem, vmem, vmem, any_spec, any_spec, any_spec, any_spec],
            out_specs=[any_spec] * 7,
            scratch_shapes=[
                pltpu.VMEM((n_seq, seq, d_model), bf16),
                pltpu.VMEM((seq, d_model), bf16),
                pltpu.VMEM((seq, n_tp * q_cols), bf16),
                pltpu.VMEM((2, d_model, q_cols + 2 * hd), bf16),
                pltpu.VMEM((2, n_tp, q_cols, nt_cols), bf16),
                pltpu.VMEM((seq, q_cols + 2 * hd), bf16),
                pltpu.VMEM((n_heads, seq, hd), bf16),
                pltpu.VMEM((seq, hd), bf16),
                pltpu.VMEM((n_seq, seq, hd), f32),
                pltpu.VMEM((n_seq, seq, hd), f32),
                pltpu.VMEM((seq, hd), f32),
                pltpu.VMEM((2, piece, hd), f32),
                dma((n_sets, 9)),
                dma((n_sets, n_tp)),
                dma((n_sets, 2)),
                dma((3, 4)),
                dma((4,)),
                dma((3, 4)),
                dma((n_tp, 4)),
                dma((4,)),
                dma((2, 3)),
                dma((2,)),
            ],
            compiler_params=pltpu.CompilerParams(
                collective_id=0, has_side_effects=True, vmem_limit_bytes=62 * 1024 * 1024),
        )(x_loc, pos, invf, norm_gain.astype(f32)[None, :], q_gain.astype(f32)[None, :],
          k_gain.astype(f32)[None, :], w_q, w_k, w_v, w_o)
        return res[0]

    return jax.shard_map(
        local_block, mesh=mesh,
        in_specs=(P('dp', 'tp', None), P('dp', 'tp'), P(None), P(None, 'tp'), P(None, 'tp'), P(None, 'tp'),
                  P(None), P(None), P('tp', None)),
        out_specs=P('dp', 'tp', None), check_vma=False)
```

time: 1310 us -> 564 us (0.43)
  waiting for transfers between devices: 712 us -> 0 us
  Pallas kernels: 0 us -> 549 us
  matrix products: 318 us -> 0 us
  other arithmetic: 196 us -> 2.59 us
  local copies, waits for them, and re-layouts: 47.3 us -> 11.3 us
  blocking collectives: 19 us -> 0 us
  between operations: 14.3 us -> 0.02 us
    pallas_call x0 -> x1, Pallas kernels: none -> 549 us  [local_block(): pl.pallas_call(body, name='attn_block', out_shape=[jax.ShapeDtypeStruct((...]
    reduce_scatter x1 -> x0, waiting for transfers between devices: 401 us -> none  [local_block(): lax.psum_scatter(head_partial, 'tp', scatter_dimension=1, tiled=True)]
    dot_general x20 -> x0, matrix products: 318 us -> none  [the longest x8 69.8 us: causal_attention(): jnp.einsum('bqkgh,btkh->bkgqt', q_block, k_rot[:, :key_len], preferred_el...]
    all_gather x1 -> x0, waiting for transfers between devices: 310 us -> none  [local_block(): full_normed = lax.all_gather(normed, 'tp', axis=1, tiled=True)]
    reduce_sum x10 -> x0, other arithmetic: 53.7 us -> none  [the longest x8 40.4 us: causal_attention(): jnp.sum(exp_scores, axis=-1, keepdims=True)]
    another operation x2 -> x0, other arithmetic: 51.6 us -> none
    cos x1 -> x0, other arithmetic: 31.9 us -> none  [rope_tables(): return (jnp.cos(angles), jnp.sin(angles))]
    mul x2 -> x0, other arithmetic: 26.6 us -> none  [rms_scale(): return vals * lax.rsqrt(mean_sq + EPS) * gain.astype(jnp.float32)]
  transfers between devices with their start and end apart: 2 -> 0, of which waited for: 2 -> 0; matrix products, arithmetic and copies ran while one was open for 3% -> 0% of each run, Pallas kernels for 0% -> 0%
where the time goes in v1:
time: 564 us; the launch traced here: 563 us
  Pallas kernels  549 us (97%)
  local copies, waits for them, and re-layouts  11.3 us (2%)
    pallas_call x1, Pallas kernels, local_block(): pl.pallas_call(body, name='attn_block', out_shape=[jax.ShapeDtypeStruct((...  549 us

profile of v1, /device:TPU:113, one launch (start us, length us, event | category | flops | bytes accessed | tf_op | source)
XLA Modules:
  0.0 562.9 jit_solution(1889997836639236048)
XLA Ops:
  0.0 0.6 maximum_bitcast_fusion.invf
  0.6 1.3 bitcast_convert_fusion
  1.9 1.3 reshape.4.ngain
  3.2 0.7 convert_element_type.4
  3.9 0.1 copy.10
  4.0 0.7 pad.4.pos_in
  4.8 548.9 %attn_block.1 = (bf16[32,64,2560]{2,1,0:T(8,128)(2,1)}, bf16[8,2560,512]{2,1,0:T(8,128)(2,1)}, bf16[8,2560,128]{2,1,0:T(8,128)(2,1)}, bf16[8,2560,128]{2,1,0:T(8...) custom-call(bf16[32,64,2560]{2,1,0:T(8,128)(2,1)} %x_in.1, ...), custom_call_target="tpu_custom_call" | custom-call | tf_op jit(solution)/shard_map/attn_block/pallas_call | solution.py:405
  553.7 9.2 %copy.12 = bf16[32,64,2560]{2,1,0:T(8,128)(2,1)} copy(bf16[32,64,2560]{2,1,0:T(8,128)(2,1)} %get-tuple-element.6) | data formatting | bytes 20971520
  (1 shorter events, 0.0 us)

commit v2 on v0

v2 whole, which is shorter than its diff:
```python
import jax
import jax.numpy as jnp
from jax import lax
from jax.experimental import pallas as pl
from jax.experimental.pallas import tpu as pltpu
from jax.sharding import PartitionSpec as P

EPS = 1e-6
THETA = 1000000.0
MESH = pl.DeviceIdType.MESH
LOG2E = 1.4426950408889634


SHARE = True


def body(x_in, pos_in, invf, ngain, qgain, kgain, wt_in, wo_in,
         out, wt_all, wo_all,
         xbuf, nbuf, obuf, wtb, wobuf, qkvt, qt, ks, vt, qcos, qsin, kcos, ksin, posbuf,
         a_send, a_recv, w_own, w_fwd, w_sib, w_pair, w_recv, w_loc, ld_sem, wo_sem):
    d_model = nbuf.shape[1]
    seq = nbuf.shape[0]
    n_seq = xbuf.shape[0]
    hd = ks.shape[1]
    q_cols = qt.shape[0]
    n_heads = q_cols // hd
    n_tp = wt_all.shape[0]
    n_dp = lax.axis_size('dp')
    share = SHARE and n_dp % 2 == 0
    chips = n_tp // 2
    piece = seq // n_tp
    dp_i = lax.axis_index('dp')
    me = lax.axis_index('tp')
    chip = me // 2
    core = me % 2

    def dev(dc, dk):
        return ((chip + dc + chips) % chips) * 2 + (core + dk) % 2

    sib = dev(0, 1)

    def rcopy(src, dst, ssem, rsem, target):
        return pltpu.make_async_remote_copy(src_ref=src, dst_ref=dst, send_sem=ssem, recv_sem=rsem,
                                            device_id=(dp_i, target), device_id_type=MESH)

    bar = pltpu.get_barrier_semaphore()
    near = [dev(dc, dk) for dc in (-1, 1, 2) for dk in (0, 1)] + [sib]
    for t in near:
        pl.semaphore_signal(bar, inc=1, device_id=(dp_i, t), device_id_type=MESH)
    par = dp_i % 2
    mate = dp_i + 1 - 2 * par
    if share:
        pl.semaphore_signal(bar, inc=1, device_id=(mate, me), device_id_type=MESH)
    pl.semaphore_wait(bar, len(near) + (1 if share else 0))

    def rows(r):
        return pl.ds(pl.multiple_of(r * piece, piece), piece)

    others = ((2, 0), (2, 1), (1, 0), (1, 1), (-1, 0), (-1, 1), (0, 1))

    def a2a_direct(a, src, dst):
        return [rcopy(src(dev(*o)), dst(me, dev(*o)), a_send.at[a, n], a_recv.at[a, me], dev(*o))
                for n, o in enumerate(others)]

    def a2a_local(a, src, dst):
        return pltpu.make_async_copy(src(me), dst(me, me), a_recv.at[a, me])

    def a2a_start(a, src, dst):
        for c in a2a_direct(a, src, dst):
            c.start()
        a2a_local(a, src, dst).start()

    def a2a_wait(a, src, dst):
        a2a_local(a, src, dst).wait()
        for o in others:
            r = dev(*o)
            ref = dst(r, me)
            rcopy(ref, ref, a_send.at[a, 0], a_recv.at[a, r], sib).wait_recv()

    def a2a_wait_sends(a, src, dst):
        for c in a2a_direct(a, src, dst):
            c.wait_send()

    def pos_src(r):
        return pos_in.at[r]

    def pos_dst(r, to):
        return posbuf.at[rows(r)]

    def x_fns(j):
        return (lambda r: x_in.at[r * n_seq + j],
                lambda r, to: xbuf.at[j, rows(r)])

    def y_fns(j):
        return (lambda r: xbuf.at[j, rows(r)],
                lambda r, to: out.at[r * n_seq + j])

    def set_x(j):
        return 1 + j

    def set_y(j):
        return 1 + n_seq + j

    Q, KV, O = range(3)

    def half(i, h):
        n = (q_cols // 2, hd, q_cols // 2)[i]
        return pl.ds(pl.multiple_of(h * n + (q_cols if i == KV else 0), n), n)

    def win(i, h):
        return (wo_in if i == O else wt_in).at[half(i, h)]

    def wref(i, h, r):
        return (wo_all if i == O else wt_all).at[r, half(i, h)]

    def w_send_own(p, which, target):
        i, h = p
        return rcopy(win(i, h), wref(i, h, me), w_own.at[which, 2 * i + h], w_recv.at[me, 2 * i + h],
                     target)

    def w_wait(p, r):
        i, h = p
        ref = wref(i, h, r)
        rcopy(ref, ref, w_own.at[0, 0], w_recv.at[r, 2 * i + h], sib).wait_recv()

    def w_to_sib(p, r, slot):
        i, h = p
        return rcopy(wref(i, h, r), wref(i, h, r), w_sib.at[slot, 2 * i + h], w_recv.at[r, 2 * i + h], sib)

    def w_onward(p, r, target):
        i, h = p
        return rcopy(wref(i, h, r), wref(i, h, r), w_fwd.at[2 * i + h], w_recv.at[r, 2 * i + h], target)

    def w_to_mate(p, r, slot):
        i, h = p
        return pltpu.make_async_remote_copy(
            src_ref=wref(i, h, r), dst_ref=wref(i, h, r), send_sem=w_pair.at[slot, 2 * i + h],
            recv_sem=w_recv.at[r, 2 * i + h], device_id=(mate, me), device_id_type=MESH)

    left, right, far = dev(-1, 0), dev(1, 0), dev(2, 0)
    L, R, F = (left, 0), (right, 1), (far, 2)
    every = [(i, h) for i in range(3) for h in range(2)]
    if share:
        first, from_mate = [(Q, par), (KV, par)], [(Q, 1 - par), (KV, 1 - par)]
    else:
        first, from_mate = [(Q, 0), (KV, 0), (Q, 1), (KV, 1)], []
    later = [(O, 0), (O, 1)]

    def got(p, src, onward=None):
        r, slot = src
        w_wait(p, r)
        if onward is not None:
            w_onward(p, r, onward).start()
        if share and p[0] != O:
            w_to_mate(p, r, slot).start()
        w_to_sib(p, r, slot).start()

    def got_mate(p, src):
        r, slot = src
        w_wait(p, r)
        w_to_sib(p, r, slot).start()

    a2a_start(0, pos_src, pos_dst)
    for p in first:
        w_send_own(p, 1, right).start()
        w_send_own(p, 2, left).start()
    for p in every:
        w_send_own(p, 0, sib).start()
    a2a_start(set_x(0), *x_fns(0))
    for p in later:
        w_send_own(p, 2, left).start()
    w_local = [pltpu.make_async_copy(wt_in, wt_all.at[me], w_loc.at[0]),
               pltpu.make_async_copy(wo_in, wo_all.at[me], w_loc.at[1])]
    for c in w_local:
        c.start()
    a2a_wait(0, pos_src, pos_dst)

    blk = 128
    lane = lax.broadcasted_iota(jnp.int32, (blk, hd), 1)

    def table_step(b, _):
        rs = pl.ds(pl.multiple_of(b * blk, blk), blk)
        for j in range(n_seq):
            ang = posbuf[rs, j:j + 1] * invf[...]
            cs = jnp.cos(ang)
            sn = jnp.sin(ang)
            sn = jnp.where(lane < hd // 2, -sn, sn)
            qcos[j, :, rs] = (cs * qgain[0:1, :]).T
            qsin[j, :, rs] = (sn * qgain[1:2, :]).T
            kcos[j, :, rs] = (cs * kgain[0:1, :]).T
            ksin[j, :, rs] = (sn * kgain[1:2, :]).T
        return 0

    lax.fori_loop(0, seq // blk, table_step, 0)

    for p in first:
        got(p, L, right)
        got(p, R)
    a2a_start(set_x(1), *x_fns(1))
    for p in later:
        w_send_own(p, 1, right).start()

    def wait_all(arrays, r):
        for i in arrays:
            for h in range(2):
                w_wait((i, h), r)

    def stage(s):
        @pl.when(s == 2)
        def _():
            for p in from_mate[:1]:
                got_mate(p, L)
                got_mate(p, R)
            for p in from_mate[1:]:
                got_mate(p, L)

        @pl.when(s == 3)
        def _():
            wait_all((Q, KV), dev(-1, 1))
            got(first[0], F)

        @pl.when(s == 4)
        def _():
            for p in from_mate[1:]:
                got_mate(p, R)
            for p in first[1:]:
                got(p, F)

        @pl.when(s == 5)
        def _():
            wait_all((Q, KV), dev(1, 1))

        @pl.when(s == 6)
        def _():
            for p in later:
                got(p, R, left)
            a2a_start(set_x(2), *x_fns(2))
            a2a_start(set_x(3), *x_fns(3))
            for p in from_mate:
                got_mate(p, F)

        @pl.when(s == 7)
        def _():
            wait_all((Q, KV), dev(2, 1))
            for c in w_local:
                c.wait()

    def gid(s):
        m = s // 2
        return ((chip + 3 * m * (m + 1) // 2) % chips) * 2 + (core + s) % 2

    def load_w(g, slot):
        return [pltpu.make_async_copy(wt_all.at[g], wtb.at[slot], ld_sem.at[slot])]

    nt_cols = wobuf.shape[3]
    n_nt = d_model // nt_cols

    def load_wo(nt, slot):
        return pltpu.make_async_copy(wo_all.at[:, :, pl.ds(pl.multiple_of(nt * nt_cols, nt_cols), nt_cols)],
                                     wobuf.at[slot], wo_sem.at[slot])

    scale2 = (hd ** -0.5) * LOG2E
    n_blk = seq // blk
    key_i = lax.broadcasted_iota(jnp.int32, (blk, 2 * blk), 0)
    qry_i = lax.broadcasted_iota(jnp.int32, (blk, 2 * blk), 1) % blk
    tri = key_i <= qry_i

    def norm_rope(row, ls, cos, sin):
        mid = hd // 2
        u1 = qkvt[row:row + mid, ls].astype(jnp.float32)
        u2 = qkvt[row + mid:row + hd, ls].astype(jnp.float32)
        r = lax.rsqrt(jnp.sum(u1 * u1 + u2 * u2, axis=0, keepdims=True) * (1.0 / hd) + EPS)
        return ((u1 * cos[:mid] + u2 * sin[:mid]) * r, (u2 * cos[mid:] + u1 * sin[mid:]) * r)

    def project(slot):
        qkvt[...] = lax.dot_general(wtb[slot], nbuf[...], (((1,), (1,)), ((), ())),
                                    preferred_element_type=jnp.float32).astype(jnp.bfloat16)

    def rope(j):
        mid = hd // 2
        for b in range(n_blk):
            ls = slice(b * blk, (b + 1) * blk)
            o1, o2 = norm_rope(q_cols, ls, kcos[j, :, ls], ksin[j, :, ls])
            ks[ls, :] = jnp.concatenate([o1, o2], axis=0).T.astype(jnp.bfloat16)
            cos, sin = qcos[j, :, ls], qsin[j, :, ls]
            for h in range(n_heads):
                o1, o2 = norm_rope(h * hd, ls, cos, sin)
                qt[h * hd:h * hd + mid, ls] = o1.astype(jnp.bfloat16)
                qt[h * hd + mid:(h + 1) * hd, ls] = o2.astype(jnp.bfloat16)
        vt[...] = qkvt[q_cols + hd:, :]

    def attend(j, g):
        oj = j % 2
        ocol = pl.multiple_of(g * q_cols, q_cols)
        for i in range(n_blk):
            kl = (i + 1) * blk
            for h in range(0, n_heads, 2):
                q2 = jnp.concatenate([qt[(h + k) * hd:(h + k + 1) * hd, i * blk:kl] for k in range(2)], axis=1)
                s = jnp.dot(ks[:kl, :], q2, preferred_element_type=jnp.float32)
                diag = jnp.where(tri, s[i * blk:, :], -jnp.inf)
                s = diag if i == 0 else jnp.concatenate([s[:i * blk, :], diag], axis=0)
                peak = jnp.max(s, axis=0, keepdims=True)
                e = jnp.exp2((s - peak) * scale2)
                inv = 1.0 / jnp.sum(e, axis=0, keepdims=True)
                p = (e * inv).astype(jnp.bfloat16)
                o = jnp.dot(vt[:, :kl], p, preferred_element_type=jnp.float32)
                for k in range(2):
                    obuf[oj, i * blk:kl, pl.ds(pl.multiple_of(ocol + (h + k) * hd, hd), hd)] = (
                        o[:, k * blk:(k + 1) * blk].T.astype(jnp.bfloat16))

    n_grp = n_tp
    n_units = n_seq * n_grp

    def normalise(j):
        a2a_wait(set_x(j), *x_fns(j))

        def n_step(r, _):
            rs = rows(r)
            xv = xbuf[j, rs, :].astype(jnp.float32)
            ms = jnp.mean(xv * xv, axis=-1, keepdims=True)
            nbuf[rs, :] = (xv * lax.rsqrt(ms + EPS) * ngain[...]).astype(jnp.bfloat16)
            return 0

        lax.fori_loop(0, n_tp, n_step, 0)

    def out_proj(j):
        def out_step(nt, _):
            ws = nt % 2
            load_wo(nt, ws).wait()

            @pl.when(nt + 1 < n_nt)
            def _():
                load_wo(nt + 1, 1 - ws).start()

            cs = pl.ds(pl.multiple_of(nt * nt_cols, nt_cols), nt_cols)
            acc = jnp.dot(obuf[j % 2], wobuf[ws].reshape(n_tp * q_cols, nt_cols), preferred_element_type=jnp.float32)
            xbuf[j, :, cs] = (xbuf[j, :, cs].astype(jnp.float32) + acc).astype(jnp.bfloat16)
            return 0

        load_wo(0, 0).start()
        lax.fori_loop(0, n_nt, out_step, 0)
        a2a_start(set_y(j), *y_fns(j))

    own_load = pltpu.make_async_copy(wt_in, wtb.at[0], ld_sem.at[0])
    own_load.start()
    wait_all((Q, KV), sib)
    for c in load_w(gid(1), 1):
        c.start()
    normalise(0)
    own_load.wait()
    project(0)

    def step(t, _):
        j, s = t // n_grp, t % n_grp
        u = t + 1

        @pl.when(j == 0)
        def _():
            stage(s + 2)

        @pl.when(jnp.logical_and(j == 1, s == 2))
        def _():
            got(later[0], L)
            got(later[0], F)

        @pl.when(jnp.logical_and(j == 1, s == 5))
        def _():
            got(later[1], L)
            got(later[1], F)

        @pl.when(u + 1 < n_units)
        def _():
            for c in load_w(gid((u + 1) % n_grp), (u + 1) % 2):
                c.start()

        @pl.when(u < n_units)
        def _():
            for c in load_w(gid(u % n_grp), u % 2):
                c.wait()

        @pl.when(s == n_grp - 1)
        def _():
            @pl.when(u < n_units)
            def _():
                normalise(j + 1)

        rope(j)
        attend(j, gid(s))
        project(u % 2)

        @pl.when(jnp.logical_and(j == 1, s == n_grp - 1))
        def _():
            wait_all((O,), sib)
            for dc in (-1, 1, 2):
                wait_all((O,), dev(dc, 1))

        @pl.when(jnp.logical_and(j > 0, s == n_grp - 1))
        def _():
            def turn(jj, _):
                out_proj(jj)
                return 0

            lax.fori_loop(j * ((j + 2) // 4), j + 1, turn, 0)

        return 0

    lax.fori_loop(0, n_units, step, 0)

    for p in every:
        w_send_own(p, 0, sib).wait_send()
        for slot, r in enumerate((left, right, far)):
            w_to_sib(p, r, slot).wait_send()
    for p in first + later:
        w_send_own(p, 1, right).wait_send()
        w_send_own(p, 2, left).wait_send()
    for p in first:
        w_onward(p, left, right).wait_send()
    for p in later:
        w_onward(p, right, left).wait_send()
    if share:
        for p in first:
            for slot, r in enumerate((left, right, far)):
                w_to_mate(p, r, slot).wait_send()
    a2a_wait_sends(0, pos_src, pos_dst)

    def end_step(j, _):
        a2a_wait_sends(set_x(j), *x_fns(j))
        a2a_wait(set_y(j), *y_fns(j))
        a2a_wait_sends(set_y(j), *y_fns(j))
        return 0

    lax.fori_loop(0, n_seq, end_step, 0)


def gain_rows(gain):
    g = gain.astype(jnp.float32)
    return jnp.stack([g, jnp.roll(g, g.shape[0] // 2)])


def solution(mesh):
    n_tp = mesh.shape['tp']

    def local_block(x_loc, pos_loc, norm_gain, w_q, w_k, w_v, q_gain, k_gain, w_o):
        batch, piece, d_model = x_loc.shape
        hd = q_gain.shape[0]
        q_cols = w_q.shape[1]
        n_seq = batch // n_tp
        seq = piece * n_tp
        f32, bf16 = jnp.float32, jnp.bfloat16
        pos = pos_loc.astype(f32).reshape(n_tp, n_seq, piece).transpose(0, 2, 1)
        pos = jnp.pad(pos, ((0, 0), (0, 0), (0, hd - n_seq)))
        inv_freq = THETA ** (-(jnp.arange(hd // 2, dtype=f32) * (2.0 / hd)))
        invf = jnp.concatenate([inv_freq, inv_freq])[None, :]
        any_spec = pl.BlockSpec(memory_space=pl.ANY)
        vmem = pl.BlockSpec(memory_space=pltpu.VMEM)
        nt_cols = 512
        dma = pltpu.SemaphoreType.DMA
        n_sets = 1 + 2 * n_seq
        w_t = jnp.concatenate([w_q, w_k, w_v], axis=1).T
        res = pl.pallas_call(
            body,
            name='attn_block',
            out_shape=[
                jax.ShapeDtypeStruct((batch, piece, d_model), bf16),
                jax.ShapeDtypeStruct((n_tp,) + w_t.shape, bf16),
                jax.ShapeDtypeStruct((n_tp,) + w_o.shape, bf16),
            ],
            in_specs=[any_spec, any_spec, vmem, vmem, vmem, vmem, any_spec, any_spec],
            out_specs=[any_spec] * 3,
            scratch_shapes=[
                pltpu.VMEM((n_seq, seq, d_model), bf16),
                pltpu.VMEM((seq, d_model), bf16),
                pltpu.VMEM((2, seq, n_tp * q_cols), bf16),
                pltpu.VMEM((2,) + w_t.shape, bf16),
                pltpu.VMEM((2, n_tp, q_cols, nt_cols), bf16),
                pltpu.VMEM((q_cols + 2 * hd, seq), bf16),
                pltpu.VMEM((q_cols, seq), bf16),
                pltpu.VMEM((seq, hd), bf16),
                pltpu.VMEM((hd, seq), bf16),
                pltpu.VMEM((n_seq, hd, seq), f32),
                pltpu.VMEM((n_seq, hd, seq), f32),
                pltpu.VMEM((n_seq, hd, seq), f32),
                pltpu.VMEM((n_seq, hd, seq), f32),
                pltpu.VMEM((seq, hd), f32),
                dma((n_sets, n_tp - 1)),
                dma((n_sets, n_tp)),
                dma((3, 6)),
                dma((6,)),
                dma((3, 6)),
                dma((3, 6)),
                dma((n_tp, 6)),
                dma((2,)),
                dma((2,)),
                dma((2,)),
            ],
            compiler_params=pltpu.CompilerParams(
                collective_id=0, has_side_effects=True, vmem_limit_bytes=62 * 1024 * 1024),
        )(x_loc, pos, invf, norm_gain.astype(f32)[None, :], gain_rows(q_gain), gain_rows(k_gain), w_t, w_o)
        return res[0]

    return jax.shard_map(
        local_block, mesh=mesh,
        in_specs=(P('dp', 'tp', None), P('dp', 'tp'), P(None), P(None, 'tp'), P(None, 'tp'), P(None, 'tp'),
                  P(None), P(None), P('tp', None)),
        out_specs=P('dp', 'tp', None), check_vma=False)
```

time: 1310 us -> 460 us (0.35)
  waiting for transfers between devices: 712 us -> 0 us
  Pallas kernels: 0 us -> 433 us
  matrix products: 318 us -> 0 us
  other arithmetic: 196 us -> 6.38 us
  local copies, waits for them, and re-layouts: 47.3 us -> 19.4 us
  blocking collectives: 19 us -> 0 us
  between operations: 14.3 us -> 0.04 us
    pallas_call x0 -> x1, Pallas kernels: none -> 433 us  [local_block(): pl.pallas_call(body, name='attn_block', out_shape=[jax.ShapeDtypeStruct((...]
    reduce_scatter x1 -> x0, waiting for transfers between devices: 401 us -> none  [local_block(): lax.psum_scatter(head_partial, 'tp', scatter_dimension=1, tiled=True)]
    dot_general x20 -> x0, matrix products: 318 us -> none  [the longest x8 69.8 us: causal_attention(): jnp.einsum('bqkgh,btkh->bkgqt', q_block, k_rot[:, :key_len], preferred_el...]
    all_gather x1 -> x0, waiting for transfers between devices: 310 us -> none  [local_block(): full_normed = lax.all_gather(normed, 'tp', axis=1, tiled=True)]
    reduce_sum x10 -> x0, other arithmetic: 53.7 us -> none  [the longest x8 40.4 us: causal_attention(): jnp.sum(exp_scores, axis=-1, keepdims=True)]
    another operation x2 -> x5, other arithmetic: 51.6 us -> 2.01 us  [gain_rows(): return jnp.stack([g, jnp.roll(g, g.shape[0] // 2)])]
    cos x1 -> x0, other arithmetic: 31.9 us -> none  [rope_tables(): return (jnp.cos(angles), jnp.sin(angles))]
    mul x2 -> x0, other arithmetic: 26.6 us -> none  [rms_scale(): return vals * lax.rsqrt(mean_sq + EPS) * gain.astype(jnp.float32)]
  transfers between devices with their start and end apart: 2 -> 0, of which waited for: 2 -> 0; matrix products, arithmetic and copies ran while one was open for 3% -> 0% of each run, Pallas kernels for 0% -> 0%
where the time goes in v2:
time: 460 us; the launch traced here: 459 us
  Pallas kernels  433 us (94%)
  local copies, waits for them, and re-layouts  19.4 us (4%)
  other arithmetic  6.38 us (1%)
    pallas_call x1, Pallas kernels, local_block(): pl.pallas_call(body, name='attn_block', out_shape=[jax.ShapeDtypeStruct((...  433 us
    unnamed x4, local copies, waits for them, and re-layouts  15.6 us

profile of v2, /device:TPU:113, one launch (start us, length us, event | category | flops | bytes accessed | tf_op | source)
XLA Modules:
  0.0 459.2 jit_solution(5627518827610140294)
XLA Ops:
  0.0 0.7 convert_bitcast_fusion.1
  0.7 0.7 convert_bitcast_fusion
  1.3 0.6 maximum_bitcast_fusion.1.invf
  1.9 0.8 fusion.1
  2.7 0.1 maximum_bitcast_fusion.2
  2.8 0.8 fusion
  3.6 0.1 maximum_bitcast_fusion.3
  3.7 0.5 pad_maximum_fusion
  4.2 1.3 reshape.4.ngain
  5.5 0.7 convert_element_type.12
  6.3 0.1 copy.13
  6.4 0.7 pad.4.pos_in
  7.2 1.3 copy.15
  8.5 2.2 copy.16
  10.7 3.0 copy.14
  13.6 3.0 maximum_bitcast_fusion.wt_in
  16.7 433.4 %attn_block.1 = (bf16[32,64,2560]{2,1,0:T(8,128)(2,1)}, bf16[8,768,2560]{2,1,0:T(8,128)(2,1)}, bf16[8,512,2560]{2,1,0:T(8,128)(2,1)}) custom-call(bf16[32,64,2560]{2,1,0:T(8,128)(2,1)} %x_in.1, f32[8,64,128]{2,1,0:T(8,128)} %pad.4.pos_in, f32[1,128]{1,0:T(1,128)} %maximum_bitcast_fusion.1.invf, f32[1,2560]{1,0:T(1,128)} %reshape.4.ngain, ...), custom_call_target="tpu_custom_call" | custom-call | tf_op jit(solution)/shard_map/attn_block/pallas_call | solution.py:460
  450.1 9.2 %copy.18 = bf16[32,64,2560]{2,1,0:T(8,128)(2,1)} copy(bf16[32,64,2560]{2,1,0:T(8,128)(2,1)} %get-tuple-element.6) | data formatting | bytes 20971520
  (1 shorter events, 0.0 us)

commit v3 on v2

--- a/solution.py
+++ b/solution.py
@@ -103,8 +103,11 @@
 
     Q, KV, O = range(3)
 
+    n_cut = (2, 2, 4)
+    base = (0, 2, 4)
+
     def half(i, h):
-        n = (q_cols // 2, hd, q_cols // 2)[i]
+        n = (q_cols // 2, hd, q_cols // 4)[i]
         return pl.ds(pl.multiple_of(h * n + (q_cols if i == KV else 0), n), n)
 
     def win(i, h):
@@ -115,43 +118,45 @@
 
     def w_send_own(p, which, target):
         i, h = p
-        return rcopy(win(i, h), wref(i, h, me), w_own.at[which, 2 * i + h], w_recv.at[me, 2 * i + h],
+        return rcopy(win(i, h), wref(i, h, me), w_own.at[which, base[i] + h], w_recv.at[me, base[i] + h],
                      target)
 
     def w_wait(p, r):
         i, h = p
         ref = wref(i, h, r)
-        rcopy(ref, ref, w_own.at[0, 0], w_recv.at[r, 2 * i + h], sib).wait_recv()
+        rcopy(ref, ref, w_own.at[0, 0], w_recv.at[r, base[i] + h], sib).wait_recv()
 
     def w_to_sib(p, r, slot):
         i, h = p
-        return rcopy(wref(i, h, r), wref(i, h, r), w_sib.at[slot, 2 * i + h], w_recv.at[r, 2 * i + h], sib)
+        return rcopy(wref(i, h, r), wref(i, h, r), w_sib.at[slot, base[i] + h], w_recv.at[r, base[i] + h], sib)
 
     def w_onward(p, r, target):
         i, h = p
-        return rcopy(wref(i, h, r), wref(i, h, r), w_fwd.at[2 * i + h], w_recv.at[r, 2 * i + h], target)
+        return rcopy(wref(i, h, r), wref(i, h, r), w_fwd.at[base[i] + h], w_recv.at[r, base[i] + h], target)
 
     def w_to_mate(p, r, slot):
         i, h = p
         return pltpu.make_async_remote_copy(
-            src_ref=wref(i, h, r), dst_ref=wref(i, h, r), send_sem=w_pair.at[slot, 2 * i + h],
-            recv_sem=w_recv.at[r, 2 * i + h], device_id=(mate, me), device_id_type=MESH)
+            src_ref=wref(i, h, r), dst_ref=wref(i, h, r), send_sem=w_pair.at[slot, base[i] + h],
+            recv_sem=w_recv.at[r, base[i] + h], device_id=(mate, me), device_id_type=MESH)
 
     left, right, far = dev(-1, 0), dev(1, 0), dev(2, 0)
     L, R, F = (left, 0), (right, 1), (far, 2)
-    every = [(i, h) for i in range(3) for h in range(2)]
+    every = [(i, h) for i in range(3) for h in range(n_cut[i])]
     if share:
         first, from_mate = [(Q, par), (KV, par)], [(Q, 1 - par), (KV, 1 - par)]
+        later, o_mate = [(O, par), (O, 2), (O, 3)], (O, 1 - par)
     else:
         first, from_mate = [(Q, 0), (KV, 0), (Q, 1), (KV, 1)], []
-    later = [(O, 0), (O, 1)]
+        later, o_mate = [(O, 0), (O, 1), (O, 2), (O, 3)], None
+    shared = first + later[:1]
 
     def got(p, src, onward=None):
         r, slot = src
         w_wait(p, r)
         if onward is not None:
             w_onward(p, r, onward).start()
-        if share and p[0] != O:
+        if share and any(p is q for q in shared):
             w_to_mate(p, r, slot).start()
         w_to_sib(p, r, slot).start()
 
@@ -169,9 +174,12 @@
     a2a_start(set_x(0), *x_fns(0))
     for p in later:
         w_send_own(p, 2, left).start()
-    w_local = [pltpu.make_async_copy(wt_in, wt_all.at[me], w_loc.at[0]),
-               pltpu.make_async_copy(wo_in, wo_all.at[me], w_loc.at[1])]
-    for c in w_local:
+    nt_cols = wobuf.shape[3]
+    n_nt = d_model // nt_cols
+    wo_cols = [slice(n * nt_cols, (n + 1) * nt_cols) for n in range(n_nt)]
+    wo_stage = [pltpu.make_async_copy(wo_in.at[:, c], wobuf.at[0, n], w_loc.at[n]) for n, c in enumerate(wo_cols)]
+    wo_place = [pltpu.make_async_copy(wobuf.at[0, n], wo_all.at[me, :, c], w_loc.at[n]) for n, c in enumerate(wo_cols)]
+    for c in wo_stage:
         c.start()
     a2a_wait(0, pos_src, pos_dst)
 
@@ -202,7 +210,7 @@
 
     def wait_all(arrays, r):
         for i in arrays:
-            for h in range(2):
+            for h in range(n_cut[i]):
                 w_wait((i, h), r)
 
     def stage(s):
@@ -242,8 +250,6 @@
         @pl.when(s == 7)
         def _():
             wait_all((Q, KV), dev(2, 1))
-            for c in w_local:
-                c.wait()
 
     def gid(s):
         m = s // 2
@@ -251,9 +257,6 @@
 
     def load_w(g, slot):
         return [pltpu.make_async_copy(wt_all.at[g], wtb.at[slot], ld_sem.at[slot])]
-
-    nt_cols = wobuf.shape[3]
-    n_nt = d_model // nt_cols
 
     def load_wo(nt, slot):
         return pltpu.make_async_copy(wo_all.at[:, :, pl.ds(pl.multiple_of(nt * nt_cols, nt_cols), nt_cols)],
@@ -289,24 +292,48 @@
                 qt[h * hd + mid:(h + 1) * hd, ls] = o2.astype(jnp.bfloat16)
         vt[...] = qkvt[q_cols + hd:, :]
 
-    def attend(j, g):
-        oj = j % 2
-        ocol = pl.multiple_of(g * q_cols, q_cols)
-        for i in range(n_blk):
-            kl = (i + 1) * blk
-            for h in range(0, n_heads, 2):
-                q2 = jnp.concatenate([qt[(h + k) * hd:(h + k + 1) * hd, i * blk:kl] for k in range(2)], axis=1)
-                s = jnp.dot(ks[:kl, :], q2, preferred_element_type=jnp.float32)
-                diag = jnp.where(tri, s[i * blk:, :], -jnp.inf)
-                s = diag if i == 0 else jnp.concatenate([s[:i * blk, :], diag], axis=0)
-                peak = jnp.max(s, axis=0, keepdims=True)
-                e = jnp.exp2((s - peak) * scale2)
-                inv = 1.0 / jnp.sum(e, axis=0, keepdims=True)
-                p = (e * inv).astype(jnp.bfloat16)
-                o = jnp.dot(vt[:, :kl], p, preferred_element_type=jnp.float32)
-                for k in range(2):
-                    obuf[oj, i * blk:kl, pl.ds(pl.multiple_of(ocol + (h + k) * hd, hd), hd)] = (
-                        o[:, k * blk:(k + 1) * blk].T.astype(jnp.bfloat16))
+    def attend_chunk(j, g, i, h):
+        kl = (i + 1) * blk
+        q2 = jnp.concatenate([qt[(h + k) * hd:(h + k + 1) * hd, i * blk:kl] for k in range(2)], axis=1)
+        s = jnp.dot(ks[:kl, :], q2, preferred_element_type=jnp.float32)
+        diag = jnp.where(tri, s[i * blk:, :], -jnp.inf)
+        s = diag if i == 0 else jnp.concatenate([s[:i * blk, :], diag], axis=0)
+        peak = jnp.max(s, axis=0, keepdims=True)
+        e = jnp.exp2((s - peak) * scale2)
+        inv = 1.0 / jnp.sum(e, axis=0, keepdims=True)
+        p = (e * inv).astype(jnp.bfloat16)
+        o = jnp.dot(vt[:, :kl], p, preferred_element_type=jnp.float32)
+        for k in range(2):
+            obuf[j % 2, i * blk:kl, pl.ds(pl.multiple_of(g * q_cols + (h + k) * hd, hd), hd)] = (
+                o[:, k * blk:(k + 1) * blk].T.astype(jnp.bfloat16))
+
+    def project_pieces(slot):
+        m_cut, k_cut = qkvt.shape[0] // 2, d_model // 10
+        for m in range(2):
+            ms = slice(m * m_cut, (m + 1) * m_cut)
+            acc = None
+            for k in range(10):
+                kc = slice(k * k_cut, (k + 1) * k_cut)
+                part = lax.dot_general(wtb[slot, ms, kc], nbuf[:, kc], (((1,), (1,)), ((), ())),
+                                       preferred_element_type=jnp.float32)
+                acc = part if acc is None else acc + part
+                if k + 1 == 10:
+                    qkvt[ms, :] = acc.astype(jnp.bfloat16)
+                yield
+
+    def attend_and_project(j, g, slot):
+        todo = [(i, h) for i in (0, 1, 2, 3) for h in range(0, n_heads, 2)]
+        pieces = 2 * 10
+        done = 0
+        steps = project_pieces(slot)
+        for n, (i, h) in enumerate(todo):
+            want = min(pieces, -(-pieces * (n + 1 + 0) // len(todo)))
+            while done < want:
+                next(steps)
+                done += 1
+            attend_chunk(j, g, i, h)
+        for _ in steps:
+            pass
 
     n_grp = n_tp
     n_units = n_seq * n_grp
@@ -348,7 +375,16 @@
         c.start()
     normalise(0)
     own_load.wait()
+    own_place = pltpu.make_async_copy(wtb.at[0], wt_all.at[me], ld_sem.at[0])
+    own_place.start()
+    for c in wo_stage:
+        c.wait()
+    for c in wo_place:
+        c.start()
     project(0)
+    own_place.wait()
+    for c in wo_place:
+        c.wait()
 
     def step(t, _):
         j, s = t // n_grp, t % n_grp
@@ -358,15 +394,19 @@
         def _():
             stage(s + 2)
 
-        @pl.when(jnp.logical_and(j == 1, s == 2))
+        @pl.when(jnp.logical_and(j == 1, s == 0))
         def _():
             got(later[0], L)
             got(later[0], F)
 
-        @pl.when(jnp.logical_and(j == 1, s == 5))
-        def _():
-            got(later[1], L)
-            got(later[1], F)
+        @pl.when(jnp.logical_and(j == 1, s == 3))
+        def _():
+            for p in later[1:]:
+                got(p, L)
+                got(p, F)
+            if share:
+                for src in (R, L, F):
+                    got_mate(o_mate, src)
 
         @pl.when(u + 1 < n_units)
         def _():
@@ -385,8 +425,7 @@
                 normalise(j + 1)
 
         rope(j)
-        attend(j, gid(s))
-        project(u % 2)
+        attend_and_project(j, gid(s), u % 2)
 
         @pl.when(jnp.logical_and(j == 1, s == n_grp - 1))
         def _():
@@ -418,7 +457,7 @@
     for p in later:
         w_onward(p, right, left).wait_send()
     if share:
-        for p in first:
+        for p in shared:
             for slot, r in enumerate((left, right, far)):
                 w_to_mate(p, r, slot).wait_send()
     a2a_wait_sends(0, pos_src, pos_dst)
@@ -484,12 +523,12 @@
                 pltpu.VMEM((seq, hd), f32),
                 dma((n_sets, n_tp - 1)),
                 dma((n_sets, n_tp)),
-                dma((3, 6)),
-                dma((6,)),
-                dma((3, 6)),
-                dma((3, 6)),
-                dma((n_tp, 6)),
-                dma((2,)),
+                dma((3, 8)),
+                dma((8,)),
+                dma((3, 8)),
+                dma((3, 8)),
+                dma((n_tp, 8)),
+                dma((8,)),
                 dma((2,)),
                 dma((2,)),
             ],

time: 460 us -> 415 us (0.902)
  Pallas kernels: 433 us -> 389 us
    pallas_call x1, Pallas kernels: 433 us -> 389 us  [local_block(): pl.pallas_call(body, name='attn_block', out_shape=[jax.ShapeDtypeStruct((...]
where the time goes in v3:
time: 415 us; the launch traced here: 414 us
  Pallas kernels  389 us (94%)
  local copies, waits for them, and re-layouts  19.4 us (5%)
  other arithmetic  6.38 us (2%)
    pallas_call x1, Pallas kernels, local_block(): pl.pallas_call(body, name='attn_block', out_shape=[jax.ShapeDtypeStruct((...  389 us
    unnamed x4, local copies, waits for them, and re-layouts  15.6 us

profile of v3, /device:TPU:113, one launch (start us, length us, event | category | flops | bytes accessed | tf_op | source)
XLA Modules:
  0.0 414.4 jit_solution(8697980319411402660)
XLA Ops:
  0.0 0.7 convert_bitcast_fusion.1
  0.7 0.7 convert_bitcast_fusion
  1.3 0.6 maximum_bitcast_fusion.1.invf
  1.9 0.8 fusion.1
  2.7 0.1 maximum_bitcast_fusion.2
  2.8 0.8 fusion
  3.6 0.1 maximum_bitcast_fusion.3
  3.7 0.5 pad_maximum_fusion
  4.2 1.3 reshape.4.ngain
  5.5 0.7 convert_element_type.12
  6.3 0.1 copy.13
  6.4 0.7 pad.4.pos_in
  7.2 1.3 copy.15
  8.5 2.2 copy.16
  10.7 3.0 copy.14
  13.6 3.0 maximum_bitcast_fusion.wt_in
  16.7 388.6 %attn_block.1 = (bf16[32,64,2560]{2,1,0:T(8,128)(2,1)}, bf16[8,768,2560]{2,1,0:T(8,128)(2,1)}, bf16[8,512,2560]{2,1,0:T(8,128)(2,1)}) custom-call(bf16[32,64,2560]{2,1,0:T(8,128)(2,1)} %x_in.1, f32[8,64,128]{2,1,0:T(8,128)} %pad.4.pos_in, f32[1,128]{1,0:T(1,128)} %maximum_bitcast_fusion.1.invf, f32[1,2560]{1,0:T(1,128)} %reshape.4.ngain, ...), custom_call_target="tpu_custom_call" | custom-call | tf_op jit(solution)/shard_map/attn_block/pallas_call | solution.py:499
  405.3 9.2 %copy.18 = bf16[32,64,2560]{2,1,0:T(8,128)(2,1)} copy(bf16[32,64,2560]{2,1,0:T(8,128)(2,1)} %get-tuple-element.6) | data formatting | bytes 20971520
  (1 shorter events, 0.0 us)

commit v4 on v3

--- a/solution.py
+++ b/solution.py
@@ -91,15 +91,16 @@
         return (lambda r: x_in.at[r * n_seq + j],
                 lambda r, to: xbuf.at[j, rows(r)])
 
-    def y_fns(j):
-        return (lambda r: xbuf.at[j, rows(r)],
-                lambda r, to: out.at[r * n_seq + j])
+    def y_fns(j, nt):
+        cs = pl.ds(pl.multiple_of(nt * nt_cols, nt_cols), nt_cols)
+        return (lambda r: xbuf.at[j, rows(r), cs],
+                lambda r, to: out.at[r * n_seq + j, :, cs])
 
     def set_x(j):
         return 1 + j
 
-    def set_y(j):
-        return 1 + n_seq + j
+    def set_y(j, nt):
+        return 1 + n_seq + j * n_nt + nt
 
     Q, KV, O = range(3)
 
@@ -186,6 +187,11 @@
     blk = 128
     lane = lax.broadcasted_iota(jnp.int32, (blk, hd), 1)
 
+    def turned(gain):
+        return pltpu.roll(jnp.broadcast_to(gain[...], (8, hd)), hd // 2, 1)[0:1]
+
+    q_gain2, k_gain2 = turned(qgain), turned(kgain)
+
     def table_step(b, _):
         rs = pl.ds(pl.multiple_of(b * blk, blk), blk)
         for j in range(n_seq):
@@ -193,10 +199,10 @@
             cs = jnp.cos(ang)
             sn = jnp.sin(ang)
             sn = jnp.where(lane < hd // 2, -sn, sn)
-            qcos[j, :, rs] = (cs * qgain[0:1, :]).T
-            qsin[j, :, rs] = (sn * qgain[1:2, :]).T
-            kcos[j, :, rs] = (cs * kgain[0:1, :]).T
-            ksin[j, :, rs] = (sn * kgain[1:2, :]).T
+            qcos[j, :, rs] = (cs * qgain[...]).T
+            qsin[j, :, rs] = (sn * q_gain2).T
+            kcos[j, :, rs] = (cs * kgain[...]).T
+            ksin[j, :, rs] = (sn * k_gain2).T
         return 0
 
     lax.fori_loop(0, seq // blk, table_step, 0)
@@ -362,11 +368,11 @@
             cs = pl.ds(pl.multiple_of(nt * nt_cols, nt_cols), nt_cols)
             acc = jnp.dot(obuf[j % 2], wobuf[ws].reshape(n_tp * q_cols, nt_cols), preferred_element_type=jnp.float32)
             xbuf[j, :, cs] = (xbuf[j, :, cs].astype(jnp.float32) + acc).astype(jnp.bfloat16)
+            a2a_start(set_y(j, nt), *y_fns(j, nt))
             return 0
 
         load_wo(0, 0).start()
         lax.fori_loop(0, n_nt, out_step, 0)
-        a2a_start(set_y(j), *y_fns(j))
 
     own_load = pltpu.make_async_copy(wt_in, wtb.at[0], ld_sem.at[0])
     own_load.start()
@@ -464,16 +470,16 @@
 
     def end_step(j, _):
         a2a_wait_sends(set_x(j), *x_fns(j))
-        a2a_wait(set_y(j), *y_fns(j))
-        a2a_wait_sends(set_y(j), *y_fns(j))
+
+        def end_cols(nt, _):
+            a2a_wait(set_y(j, nt), *y_fns(j, nt))
+            a2a_wait_sends(set_y(j, nt), *y_fns(j, nt))
+            return 0
+
+        lax.fori_loop(0, n_nt, end_cols, 0)
         return 0
 
     lax.fori_loop(0, n_seq, end_step, 0)
-
-
-def gain_rows(gain):
-    g = gain.astype(jnp.float32)
-    return jnp.stack([g, jnp.roll(g, g.shape[0] // 2)])
 
 
 def solution(mesh):
@@ -494,7 +500,7 @@
         vmem = pl.BlockSpec(memory_space=pltpu.VMEM)
         nt_cols = 512
         dma = pltpu.SemaphoreType.DMA
-        n_sets = 1 + 2 * n_seq
+        n_sets = 1 + n_seq + n_seq * (d_model // nt_cols)
         w_t = jnp.concatenate([w_q, w_k, w_v], axis=1).T
         res = pl.pallas_call(
             body,
@@ -534,7 +540,7 @@
             ],
             compiler_params=pltpu.CompilerParams(
                 collective_id=0, has_side_effects=True, vmem_limit_bytes=62 * 1024 * 1024),
-        )(x_loc, pos, invf, norm_gain.astype(f32)[None, :], gain_rows(q_gain), gain_rows(k_gain), w_t, w_o)
+        )(x_loc, pos, invf, norm_gain.astype(f32)[None, :], q_gain.astype(f32)[None, :], k_gain.astype(f32)[None, :], w_t, w_o)
         return res[0]
 
     return jax.shard_map(

time: 415 us -> 407 us (0.981)
  Pallas kernels: 389 us -> 383 us
    pallas_call x1, Pallas kernels: 389 us -> 383 us  [local_block(): pl.pallas_call(body, name='attn_block', out_shape=[jax.ShapeDtypeStruct((...]
where the time goes in v4:
time: 407 us; the launch traced here: 406 us
  Pallas kernels  383 us (94%)
  local copies, waits for them, and re-layouts  17.8 us (4%)
  other arithmetic  5.58 us (1%)
    pallas_call x1, Pallas kernels, local_block(): pl.pallas_call(body, name='attn_block', out_shape=[jax.ShapeDtypeStruct((...  383 us
    unnamed x4, local copies, waits for them, and re-layouts  15.6 us

profile of v4, /device:TPU:113, one launch (start us, length us, event | category | flops | bytes accessed | tf_op | source)
XLA Modules:
  0.0 406.4 jit_solution(8604990745142475845)
XLA Ops:
  0.0 0.6 maximum_bitcast_fusion.1.invf
  0.6 1.2 bitcast_convert_fusion
  1.8 1.3 reshape.4.ngain
  3.1 0.7 convert_element_type.4
  3.8 0.1 copy.13
  4.0 0.7 pad.4.pos_in
  4.7 1.3 copy.15
  6.1 2.2 copy.16
  8.2 3.0 copy.14
  11.2 3.0 maximum_bitcast_fusion.wt_in
  14.2 383.0 %attn_block.1 = (bf16[32,64,2560]{2,1,0:T(8,128)(2,1)}, bf16[8,768,2560]{2,1,0:T(8,128)(2,1)}, bf16[8,512,2560]{2,1,0:T(8,128)(2,1)}) custom-call(bf16[32,64,2560]{2,1,0:T(8,128)(2,1)} %x_in.1, f32[8,64,128]{2,1,0:T(8,128)} %pad.4.pos_in, f32[1,128]{1,0:T(1,128)} %maximum_bitcast_fusion.1.invf, f32[1,2560]{1,0:T(1,128)} %reshape.4.ngain, ...), custom_call_target="tpu_custom_call" | custom-call | tf_op jit(solution)/shard_map/attn_block/pallas_call | solution.py:505
  397.2 9.2 %copy.18 = bf16[32,64,2560]{2,1,0:T(8,128)(2,1)} copy(bf16[32,64,2560]{2,1,0:T(8,128)(2,1)} %get-tuple-element.6) | data formatting | bytes 20971520
  (1 shorter events, 0.0 us)
